TPU v7x, 32 devices: a whole 2x2x4 slice. The times are simulated.
32 devices in a mesh: gx: 2 (over core), gy: 4 (over y, x), gz: 4 (over z).
Axes of the slice: x: 2, y: 2, z: 4, core: 2. Of those that a mesh axis runs over, the one named last changes fastest.
Arguments:
- right_side: float32 [96, 192, 192], P('gx', 'gy', 'gz'), may hold values from -6 to 6
- face_coef: float32 [3, 96, 192, 192], P(None, 'gx', 'gy', 'gz'), may hold values from 0.3 to 3
- absorption: float32 [96, 192, 192], P('gx', 'gy', 'gz'), may hold values from 0.001 to 0.01
Outputs:
- solution: float32 [96, 192, 192], P('gx', 'gy', 'gz')
- residual: float32 [96, 192, 192], P('gx', 'gy', 'gz')
- relative_norm: float32 [], replicated
All inputs are finite; a program needn't handle non-finite values.
Results may differ from a plain program's by a relative error of at most 0.0003.
Values sent between devices are 32-bit elements.
A program may use at most 192 MiB of HBM per device.

v0:
```python
import jax
import jax.numpy as jnp
from jax import lax
from jax.sharding import PartitionSpec as P

LEVELS = 5
SWEEPS = 3
BOTTOM = 6


cheb_low = 0.25
cheb_high = 2.0


def with_halo(value, sides, width, wrap):
    for axis, dim in sides:
        devices, length = lax.axis_size(axis), value.shape[dim]
        up = [(i, (i + 1) % devices) for i in range(devices if wrap else devices - 1)]
        down = [(j, i) for i, j in up]
        last = lax.slice_in_dim(value, length - width, length, axis=dim)
        leading = lax.slice_in_dim(value, 0, width, axis=dim)
        before = lax.ppermute(last, axis, up)
        after = lax.ppermute(leading, axis, down)
        value = jnp.concatenate([before, value, after], axis=dim)
    return value


def from_behind(value, axis, by):
    devices = lax.axis_size(axis)
    pairs = [(i, i + by) for i in range(devices) if 0 <= i + by < devices]
    return lax.ppermute(value, axis, pairs)


def apply_stencil(field, stencil, weight, padded):
    low_x = padded[:-2, 1:-1, 1:-1]
    high_x = padded[2:, 1:-1, 1:-1]
    low_y = padded[1:-1, :-2, 1:-1]
    high_y = padded[1:-1, 2:, 1:-1]
    low_z = padded[1:-1, 1:-1, :-2]
    high_z = padded[1:-1, 1:-1, 2:]
    flux = stencil[0] * (field - low_x) + stencil[3] * (field - high_x)
    flux = flux + stencil[1] * (field - low_y) + stencil[4] * (field - high_y)
    flux = flux + stencil[2] * (field - low_z) + stencil[5] * (field - high_z)
    return stencil[6] * field + weight * flux


def inverse_diagonal(stencil, weight):
    total = stencil[0] + stencil[3] + stencil[1] + stencil[4] + stencil[2] + stencil[5]
    return 1.0 / (stencil[6] + weight * total)


def chebyshev(iterate, source, stencil, weight, sweeps, from_zero, pad_field):
    centre = 0.5 * (cheb_high + cheb_low)
    half_width = 0.5 * (cheb_high - cheb_low)
    cheb_ratio = centre / half_width
    cheb_rho = 1.0 / cheb_ratio
    scaling = inverse_diagonal(stencil, weight)
    if from_zero:
        remainder = source
    else:
        remainder = source - apply_stencil(iterate, stencil, weight, pad_field(iterate))
    update = scaling * remainder * (1.0 / centre)
    for sweep in range(sweeps):
        iterate = iterate + update
        if sweep + 1 < sweeps:
            remainder = source - apply_stencil(iterate, stencil, weight, pad_field(iterate))
            next_rho = 1.0 / (2.0 * cheb_ratio - cheb_rho)
            update = next_rho * cheb_rho * update + 2.0 * next_rho / half_width * (
                scaling * remainder
            )
            cheb_rho = next_rho
    return iterate


def conjugate(source, stencil, weight, pad_field, total):
    iterate = jnp.zeros_like(source)
    remainder = source
    search = source
    norm_now = total(remainder * remainder)
    for step in range(BOTTOM):
        applied = apply_stencil(search, stencil, weight, pad_field(search))
        step_size = norm_now / total(search * applied)
        iterate = iterate + step_size * search
        if step + 1 < BOTTOM:
            remainder = remainder - step_size * applied
            norm_next = total(remainder * remainder)
            search = remainder + norm_next / norm_now * search
            norm_now = norm_next
    return iterate


def average_cells(field):
    blocks = field.reshape(field.shape[0] // 2, 2, field.shape[1] // 2, 2, field.shape[2] // 2, 2)
    return jnp.sum(blocks, axis=(1, 3, 5)) * 0.125


def average_faces(faces):
    halves = (faces.shape[1] // 2, 2, faces.shape[2] // 2, 2, faces.shape[3] // 2, 2)
    along_x = faces[0].reshape(halves)[:, 0]
    along_y = faces[1].reshape(halves)[:, :, :, 0]
    along_z = faces[2].reshape(halves)[..., 0]
    return (
        jnp.stack(
            [
                jnp.sum(along_x, axis=(2, 4)),
                jnp.sum(along_y, axis=(1, 4)),
                jnp.sum(along_z, axis=(1, 3)),
            ]
        )
        * 0.25
    )


def repeat_cells(field):
    shape = field.shape
    wide = jnp.broadcast_to(
        field[:, None, :, None, :, None], (shape[0], 2, shape[1], 2, shape[2], 2)
    )
    return wide.reshape(2 * shape[0], 2 * shape[1], 2 * shape[2])


def pad_zero(field):
    return jnp.pad(field, 1)


def halo_field(field):
    return with_halo(field, (("gx", 0), ("gy", 1), ("gz", 2)), 1, False)


def prepare(faces, cells):
    above_x = from_behind(faces[0, :1], "gx", -1)
    above_y = from_behind(faces[1, :, :1], "gy", -1)
    above_z = from_behind(faces[2, :, :, :1], "gz", -1)
    high_x = jnp.concatenate([faces[0, 1:], above_x], axis=0)
    high_y = jnp.concatenate([faces[1, :, 1:], above_y], axis=1)
    high_z = jnp.concatenate([faces[2, :, :, 1:], above_z], axis=2)
    return jnp.stack([faces[0], faces[1], faces[2], high_x, high_y, high_z, cells])


def assemble(flat, count, block):
    count_x = lax.axis_size("gx")
    count_y = lax.axis_size("gy")
    count_z = lax.axis_size("gz")
    grid = flat.reshape(count_x, count_y, count_z, count, block[0], block[1], block[2])
    grid = jnp.transpose(grid, (3, 0, 4, 1, 5, 2, 6))
    return grid.reshape(count, count_x * block[0], count_y * block[1], count_z * block[2])


def body(right_side, face_coef, absorption):
    source_sq = lax.psum(jnp.sum(right_side * right_side), ("gx", "gy", "gz"))
    stencils = []
    faces = face_coef
    cells = absorption
    for level in range(LEVELS):
        stencils.append(prepare(faces, cells))
        if level + 1 < LEVELS:
            faces = average_faces(faces)
            cells = average_cells(cells)
    sources = []
    iterates = []
    source = right_side
    for level in range(LEVELS - 1):
        weight = 0.25**level
        iterate = chebyshev(
            jnp.zeros_like(source), source, stencils[level], weight, SWEEPS, True, halo_field
        )
        remainder = source - apply_stencil(iterate, stencils[level], weight, halo_field(iterate))
        sources.append(source)
        iterates.append(iterate)
        source = average_cells(remainder)
    coarse = stencils[LEVELS - 1]
    block = source.shape
    weight_low = 0.25 ** (LEVELS - 1)
    flat_coef = lax.all_gather(coarse.reshape(-1), ("gx", "gy", "gz"), axis=0, tiled=True)
    flat_source = lax.all_gather(source.reshape(-1), ("gx", "gy", "gz"), axis=0, tiled=True)
    whole_coef = assemble(flat_coef, 7, block)
    whole_source = assemble(flat_source, 1, block)[0]
    whole = conjugate(whole_source, whole_coef, weight_low, pad_zero, jnp.sum)
    starts = (
        lax.axis_index("gx") * block[0],
        lax.axis_index("gy") * block[1],
        lax.axis_index("gz") * block[2],
    )
    correction = lax.dynamic_slice(whole, starts, block)
    for level in reversed(range(LEVELS - 1)):
        weight = 0.25**level
        iterate = iterates[level] + repeat_cells(correction)
        correction = chebyshev(
            iterate, sources[level], stencils[level], weight, SWEEPS, False, halo_field
        )
    residual = right_side - apply_stencil(correction, stencils[0], 1.0, halo_field(correction))
    residual_sq = lax.psum(jnp.sum(residual * residual), ("gx", "gy", "gz"))
    relative_norm = jnp.sqrt(residual_sq / source_sq)
    return (correction, residual, relative_norm)


def solution(mesh):
    return jax.shard_map(
        body,
        mesh=mesh,
        in_specs=(P("gx", "gy", "gz"), P(None, "gx", "gy", "gz"), P("gx", "gy", "gz")),
        out_specs=(P("gx", "gy", "gz"), P("gx", "gy", "gz"), P()),
        check_vma=False,
    )
```

profile of v0, /device:TPU:0, one launch (start us, length us, event | category | flops | bytes accessed | tf_op | source)
XLA Modules:
  0.0 1281.1 jit_solution(7671613528948734869)
XLA Ops:
  14.1 15.2 %reshape_squeeze.37 = f32[24,2,24,2,24,2]{5,4,3,2,1,0:T(8,128)} reshape(f32[1,48,48,48]{3,2,1,0:T(8,128)} %get-tuple-element.63) | data formatting | bytes 884736 | tf_op jit(solution)/shard_map/reshape;squeeze | solution.py:100
  29.3 7.7 slice_reduce_fusion.1
  37.0 15.2 %reshape_squeeze.38 = f32[24,2,24,2,24,2]{5,4,3,2,1,0:T(8,128)} reshape(f32[1,48,48,48]{3,2,1,0:T(8,128)} %get-tuple-element.62) | data formatting | bytes 884736 | tf_op jit(solution)/shard_map/reshape;squeeze | solution.py:101
  52.2 11.8 slice_reduce_fusion
  64.0 15.2 %reshape_squeeze.36 = f32[24,2,24,2,24,2]{5,4,3,2,1,0:T(8,128)} reshape(f32[1,48,48,48]{3,2,1,0:T(8,128)} %get-tuple-element.61) | data formatting | bytes 884736 | tf_op jit(solution)/shard_map/reshape;squeeze | solution.py:99
  79.3 7.0 slice_reduce_fusion.2
  124.2 5.8 multiply_multiply_fusion
  136.7 6.2 collective-permute-start.5
  154.6 5.6 collective-permute-start.7
  171.2 12.1 multiply_add_fusion.1
  189.8 5.4 collective-permute-start.11
  207.3 4.4 collective-permute-start.13
  224.2 11.4 fusion.111
  259.6 5.1 collective-permute-start.22
  270.1 15.2 %reshape.86 = f32[24,2,24,2,24,2]{5,4,3,2,1,0:T(8,128)} reshape(f32[48,48,48]{2,1,0:T(8,128)} %param.5) | data formatting | bytes 884736 | tf_op jit(solution)/shard_map/reshape | solution.py:93
  286.6 10.9 reduce_sum.306
  305.2 11.5 fusion.88
  316.7 15.2 %reshape.87 = f32[24,2,24,2,24,2]{5,4,3,2,1,0:T(8,128)} reshape(f32[48,48,48]{2,1,0:T(8,128)} %fusion.88) | data formatting | bytes 884736 | tf_op jit(solution)/shard_map/reshape | solution.py:93
  331.9 10.9 reduce_sum.310
  353.6 4.5 collective-permute-start.26
  364.6 5.2 collective-permute-start.28
  371.7 6.3 collective-permute-done.28
  388.7 4.5 collective-permute-start.32
  400.0 4.9 collective-permute-start.34
  412.3 5.0 collective-permute-done.35
  493.0 5.2 collective-permute-start.49
  511.0 4.6 collective-permute-start.53
  528.8 4.5 collective-permute-done.56
  585.2 4.8 collective-permute-start.68
  591.4 4.5 collective-permute-done.69
  596.7 5.2 collective-permute-start.70
  613.9 4.4 collective-permute-start.74
  624.5 4.5 collective-permute-start.76
  670.9 41.3 %all-reduce.9 = (f32[6048]{0:T(1024)}, f32[864]{0:T(1024)}) all-reduce(f32[6048]{0:T(1024)} %dynamic-update-slice.1, f32[864]{0:T(1024)} %dynamic-update-slice), channel_id=1, replica_groups=mesh['gx'=2,'gy'=4,'gz'=4] {'gx','gy','gz'}, use_global_device_ids=true, to_apply=%add.7 | all-reduce | flops 6912 | bytes 55296
  822.4 4.4 collective-permute-start.95
  887.4 4.3 collective-permute-done.110
  909.9 4.3 collective-permute-done.116
  932.4 4.3 collective-permute-done.122
  962.4 6.6 collective-permute-done.127
  991.4 6.6 collective-permute-done.133
  1020.5 6.6 collective-permute-done.139
  1032.6 9.6 broadcast_in_dim.11
  1042.2 17.3 %reshape.97 = f32[48,48,48]{2,1,0:T(8,128)} reshape(f32[24,2,24,2,24,2]{5,4,3,2,1,0:T(8,128)} %broadcast_in_dim.11) | data formatting | bytes 884736 | tf_op jit(solution)/shard_map/reshape | solution.py:119
  1093.7 11.9 multiply_add_fusion
  1137.9 12.8 %fusion.292 = (f32[48,48,48]{2,1,0:T(8,128)S(1)}, f32[48,48,48]{2,1,0:T(8,128)}) fusion(f32[48,48,48]{2,1,0:T(8,128)} %copy-done.10, f32[48,48,48]{2,1,0:T(8,128)} %get-tuple-element.12, f32[48,48,48]{2,1,0:T(8,128)} %get-tuple-element.59, f32[48,48,48]{2,1,0:T(8,128)} %param.3, f32[48,48,48]{2,1,0:T(8,128)} %get-tuple-element.60, ...), kind=kLoop, calls=%fused_computation.578 | loop fusion | flops 5197824 | bytes 6250784 | tf_op jit(solution)/shard_map/add | solution.py:64
  1183.4 11.1 fusion.27
  1226.9 13.0 %multiply_reduce_fusion.1 = (f32[]{:T(128)}, f32[48,48,48]{2,1,0:T(8,128)}) fusion(f32[48,48,48]{2,1,0:T(8,128)} %param.3, f32[48,48,48]{2,1,0:T(8,128)} %get-tuple-element.60, f32[48,48,48]{2,1,0:T(8,128)} %copy-done.15, f32[50,50,1]{2,1,0:T(8,128)} %copy.196, f32[50,1,48]{2,1,0:T(1,128)} %copy-done.85, f32[1,48,48]{2,1,0:T(8,128)} %copy-done.72, ...), kind=kLoop, calls=%fused_computation.298 | loop fusion | flops 4644863 | bytes 4481316 | tf_op jit(solution)/shard_map/reduce_sum | solution.py:192
  1239.9 38.4 %all-reduce.8 = (f32[]{:T(128)}, f32[]{:T(128)}) all-reduce(f32[]{:T(128)} %get-tuple-element.7, f32[]{:T(128)} %get-tuple-element.99), channel_id=1, replica_groups=mesh['gx'=2,'gy'=4,'gz'=4] {'gx','gy','gz'}, use_global_device_ids=true, to_apply=%region_33.34 | all-reduce | flops 2 | bytes 16 | tf_op jit(solution)/shard_map/psum | solution.py:192
  (818 shorter events, 807.1 us)
Async XLA Ops:
  2.0 122.2 %collective-permute-start = (f32[1,48,48]{2,1,0:T(8,128)}, f32[1,48,48]{2,1,0:T(8,128)}, u32[]{:S(2)}, u32[]{:S(2)}) collective-permute-start(f32[1,48,48]{2,1,0:T(8,128)} %slice_bitcast_fusion.13), channel_id=1, source_target_pairs={{16,0},{17,1},{18,2},{19,3},{20,4},{21,5},{22,6},{23,7},{24,8},{25... | collective-permute-start | bytes 27656 | tf_op jit(solution)/shard_map/ppermute | solution.py:31
  4.8 119.4 %collective-permute-start.1 = (f32[48,1,48]{2,1,0:T(1,128)}, f32[48,1,48]{2,1,0:T(1,128)}, u32[]{:S(2)}, u32[]{:S(2)}) collective-permute-start(f32[48,1,48]{2,1,0:T(1,128)} %slice_bitcast_fusion.12), channel_id=1, source_target_pairs={{4,0},{8,4},{12,8},{5,1},{9,5},{13,9},{6,2},{10,6},{14,10},{7,3},{... | collective-permute-start | bytes 27656 | tf_op jit(solution)/shard_map/ppermute | solution.py:31
  10.9 109.8 %collective-permute-start.2 = (f32[48,48,1]{1,0,2:T(8,128)}, f32[48,48,1]{1,0,2:T(8,128)}, u32[]{:S(2)}, u32[]{:S(2)}) collective-permute-start(f32[48,48,1]{1,0,2:T(8,128)} %bitcast.310), channel_id=1, source_target_pairs={{1,0},{2,1},{3,2},{5,4},{6,5},{7,6},{9,8},{10,9},{11,10},{13,12},{... | collective-permute-start | bytes 27656 | tf_op jit(solution)/shard_map/ppermute | solution.py:31
  87.1 255.7 %collective-permute-start.15 = (f32[1,24,24]{2,1,0:T(8,128)}, f32[1,24,24]{2,1,0:T(8,128)S(1)}, u32[]{:S(2)}, u32[]{:S(2)}) collective-permute-start(f32[1,24,24]{2,1,0:T(8,128)} %slice_bitcast_fusion.16), channel_id=1, source_target_pairs={{16,0},{17,1},{18,2},{19,3},{20,4},{21,5},{22,6},{23,7},{24,8},{25... | collective-permute-start | bytes 6920 | tf_op jit(solution)/shard_map/ppermute | solution.py:31
  88.9 255.3 %collective-permute-start.16 = (f32[24,1,24]{2,1,0:T(1,128)}, f32[24,1,24]{2,1,0:T(1,128)}, u32[]{:S(2)}, u32[]{:S(2)}) collective-permute-start(f32[24,1,24]{2,1,0:T(1,128)} %slice_bitcast_fusion.15), channel_id=1, source_target_pairs={{4,0},{8,4},{12,8},{5,1},{9,5},{13,9},{6,2},{10,6},{14,10},{7,3},{... | collective-permute-start | bytes 6920 | tf_op jit(solution)/shard_map/ppermute | solution.py:31
  120.7 223.6 %collective-permute-start.17 = (f32[24,24,1]{2,1,0:T(8,128)}, f32[24,24,1]{2,1,0:T(8,128)}, u32[]{:S(2)}, u32[]{:S(2)}) collective-permute-start(f32[24,24,1]{2,1,0:T(8,128)} %slice_bitcast_fusion.3), channel_id=1, source_target_pairs={{1,0},{2,1},{3,2},{5,4},{6,5},{7,6},{9,8},{10,9},{11,10},{13,12},{... | collective-permute-start | bytes 6920 | tf_op jit(solution)/shard_map/ppermute | solution.py:31
  136.7 8.2 collective-permute-start.5
  154.6 10.9 collective-permute-start.7
  189.8 9.9 collective-permute-start.11
  207.3 12.0 collective-permute-start.13
  214.2 7.6 collective-permute-start.14
  259.6 37.9 %collective-permute-start.22 = (f32[50,50,1]{1,2,0:T(1,128)}, f32[50,50,1]{1,2,0:T(1,128)}, u32[]{:S(2)}, u32[]{:S(2)}) collective-permute-start(f32[50,50,1]{1,2,0:T(1,128)} %copy.162), channel_id=1, source_target_pairs={{0,1},{1,2},{2,3},{4,5},{5,6},{6,7},{8,9},{9,10},{10,11},{12,13},{... | collective-permute-start | bytes 30008 | tf_op jit(solution)/shard_map/ppermute | solution.py:22
  267.2 34.0 %collective-permute-start.23 = (f32[50,50,1]{1,2,0:T(1,128)}, f32[50,50,1]{1,2,0:T(1,128)}, u32[]{:S(2)}, u32[]{:S(2)}) collective-permute-start(f32[50,50,1]{1,2,0:T(1,128)} %copy.164), channel_id=1, source_target_pairs={{1,0},{2,1},{3,2},{5,4},{6,5},{7,6},{9,8},{10,9},{11,10},{13,12},{... | collective-permute-start | bytes 30008 | tf_op jit(solution)/shard_map/ppermute | solution.py:23
  297.5 176.9 %collective-permute-start.36 = (f32[1,12,12]{2,1,0:T(8,128)}, f32[1,12,12]{2,1,0:T(8,128)}, u32[]{:S(2)}, u32[]{:S(2)}) collective-permute-start(f32[1,12,12]{2,1,0:T(8,128)} %slice_bitcast_fusion.17), channel_id=1, source_target_pairs={{16,0},{17,1},{18,2},{19,3},{20,4},{21,5},{22,6},{23,7},{24,8},{25... | collective-permute-start | bytes 1736 | tf_op jit(solution)/shard_map/ppermute | solution.py:31
  301.2 173.1 %collective-permute-start.37 = (f32[12,1,12]{2,1,0:T(1,128)}, f32[12,1,12]{2,1,0:T(1,128)}, u32[]{:S(2)}, u32[]{:S(2)}) collective-permute-start(f32[12,1,12]{2,1,0:T(1,128)} %slice_bitcast_fusion.18), channel_id=1, source_target_pairs={{4,0},{8,4},{12,8},{5,1},{9,5},{13,9},{6,2},{10,6},{14,10},{7,3},{... | collective-permute-start | bytes 1736 | tf_op jit(solution)/shard_map/ppermute | solution.py:31
  342.8 106.3 %collective-permute-start.38 = (f32[12,12,1]{1,2,0:T(1,128)}, f32[12,12,1]{1,2,0:T(1,128)}, u32[]{:S(2)}, u32[]{:S(2)}) collective-permute-start(f32[12,12,1]{1,2,0:T(1,128)} %squeeze.175), channel_id=1, source_target_pairs={{1,0},{2,1},{3,2},{5,4},{6,5},{7,6},{9,8},{10,9},{11,10},{13,12},{... | collective-permute-start | bytes 1736 | tf_op jit(solution)/shard_map/ppermute | solution.py:31
  364.6 13.4 %collective-permute-start.28 = (f32[26,26,1]{2,1,0:T(8,128)S(1)}, f32[26,26,1]{2,1,0:T(8,128)S(1)}, u32[]{:S(2)}, u32[]{:S(2)}) collective-permute-start(f32[26,26,1]{2,1,0:T(8,128)S(1)} %get-tuple-element.127), channel_id=1, source_target_pairs={{0,1},{1,2},{2,3},{4,5},{5,6},{6,7},{8,9},{9,10},{10,11},{12,13},{... | collective-permute-start | bytes 8120 | tf_op jit(solution)/shard_map/ppermute | solution.py:22
  369.8 12.4 collective-permute-start.29
  400.0 12.3 collective-permute-start.34
  404.9 12.4 collective-permute-start.35
  440.0 19.5 %collective-permute-start.43 = (f32[26,26,1]{2,1,0:T(8,128)}, f32[26,26,1]{2,1,0:T(8,128)}, u32[]{:S(2)}, u32[]{:S(2)}) collective-permute-start(f32[26,26,1]{2,1,0:T(8,128)} %get-tuple-element.123), channel_id=1, source_target_pairs={{0,1},{1,2},{2,3},{4,5},{5,6},{6,7},{8,9},{9,10},{10,11},{12,13},{... | collective-permute-start | bytes 8120 | tf_op jit(solution)/shard_map/ppermute | solution.py:22
  443.6 17.2 %collective-permute-start.44 = (f32[26,26,1]{2,1,0:T(8,128)}, f32[26,26,1]{2,1,0:T(8,128)}, u32[]{:S(2)}, u32[]{:S(2)}) collective-permute-start(f32[26,26,1]{2,1,0:T(8,128)} %get-tuple-element.124), channel_id=1, source_target_pairs={{1,0},{2,1},{3,2},{5,4},{6,5},{7,6},{9,8},{10,9},{11,10},{13,12},{... | collective-permute-start | bytes 8120 | tf_op jit(solution)/shard_map/ppermute | solution.py:23
  449.1 108.3 %collective-permute-start.57 = (f32[1,6,6]{2,0,1:T(1,128)}, f32[1,6,6]{2,0,1:T(1,128)}, u32[]{:S(2)}, u32[]{:S(2)}) collective-permute-start(f32[1,6,6]{2,0,1:T(1,128)} %squeeze.177), channel_id=1, source_target_pairs={{16,0},{17,1},{18,2},{19,3},{20,4},{21,5},{22,6},{23,7},{24,8},{25... | collective-permute-start | bytes 440 | tf_op jit(solution)/shard_map/ppermute | solution.py:31
  459.5 113.9 %collective-permute-start.58 = (f32[6,1,6]{2,1,0:T(1,128)}, f32[6,1,6]{2,1,0:T(1,128)}, u32[]{:S(2)}, u32[]{:S(2)}) collective-permute-start(f32[6,1,6]{2,1,0:T(1,128)} %slice_bitcast_fusion.20), channel_id=1, source_target_pairs={{4,0},{8,4},{12,8},{5,1},{9,5},{13,9},{6,2},{10,6},{14,10},{7,3},{... | collective-permute-start | bytes 440 | tf_op jit(solution)/shard_map/ppermute | solution.py:31
  460.8 98.6 %collective-permute-start.59 = (f32[6,6,1]{1,2,0:T(1,128)}, f32[6,6,1]{1,2,0:T(1,128)}, u32[]{:S(2)}, u32[]{:S(2)}) collective-permute-start(f32[6,6,1]{1,2,0:T(1,128)} %squeeze.181), channel_id=1, source_target_pairs={{1,0},{2,1},{3,2},{5,4},{6,5},{7,6},{9,8},{10,9},{11,10},{13,12},{... | collective-permute-start | bytes 440 | tf_op jit(solution)/shard_map/ppermute | solution.py:31
  493.0 7.5 collective-permute-start.49
  521.9 6.8 collective-permute-start.55
  526.2 7.0 collective-permute-start.56
  543.1 7.8 collective-permute-start.62
  554.1 11.7 collective-permute-start.64
  556.1 10.9 collective-permute-start.65
  557.4 62.2 %collective-permute-start.86 = (f32[3,3,1]{1,2,0:T(1,128)}, f32[3,3,1]{1,2,0:T(1,128)}, u32[]{:S(2)}, u32[]{:S(2)}) collective-permute-start(f32[3,3,1]{1,2,0:T(1,128)} %squeeze.187), channel_id=1, source_target_pairs={{1,0},{2,1},{3,2},{5,4},{6,5},{7,6},{9,8},{10,9},{11,10},{13,12},{... | collective-permute-start | bytes 116 | tf_op jit(solution)/shard_map/ppermute | solution.py:31
  559.4 43.8 %collective-permute-start.84 = (f32[1,3,3]{2,0,1:T(1,128)}, f32[1,3,3]{2,0,1:T(1,128)}, u32[]{:S(2)}, u32[]{:S(2)}) collective-permute-start(f32[1,3,3]{2,0,1:T(1,128)} %squeeze.183), channel_id=1, source_target_pairs={{16,0},{17,1},{18,2},{19,3},{20,4},{21,5},{22,6},{23,7},{24,8},{25... | collective-permute-start | bytes 116 | tf_op jit(solution)/shard_map/ppermute | solution.py:31
  565.7 64.6 %collective-permute-start.85 = (f32[3,1,3]{2,1,0:T(1,128)}, f32[3,1,3]{2,1,0:T(1,128)}, u32[]{:S(2)}, u32[]{:S(2)}) collective-permute-start(f32[3,1,3]{2,1,0:T(1,128)} %slice_bitcast_fusion.21), channel_id=1, source_target_pairs={{4,0},{8,4},{12,8},{5,1},{9,5},{13,9},{6,2},{10,6},{14,10},{7,3},{... | collective-permute-start | bytes 116 | tf_op jit(solution)/shard_map/ppermute | solution.py:31
  596.7 7.2 collective-permute-start.70
  613.9 6.9 collective-permute-start.74
  624.5 8.5 collective-permute-start.76
  641.5 7.7 collective-permute-start.80
  652.2 9.1 collective-permute-start.82
  959.1 9.9 collective-permute-start.127
  961.1 12.1 collective-permute-start.128
  987.9 10.1 collective-permute-start.133
  990.1 12.1 collective-permute-start.134
  1016.9 10.1 collective-permute-start.139
  1019.2 12.1 collective-permute-start.140
  1124.0 7.1 collective-permute-start.151
  1169.2 7.1 collective-permute-start.157
  1213.0 6.8 collective-permute-start.163
  (229 other events, 2313.7 us)
where the time goes:
time: 1300 us; the launch traced here: 1280 us
  local copies, waits for them, and re-layouts  345 us (27%)
  starting transfers between devices  344 us (26%)
  other arithmetic  259 us (20%)
  waiting for transfers between devices  232 us (18%)
  blocking collectives  79.7 us (6%)
  between operations  21.3 us (2%)
    ppermute x75, starting transfers between devices, with_halo(): before = lax.ppermute(last, axis, up)  226 us
    ppermute x75, waiting for transfers between devices, with_halo(): after = lax.ppermute(leading, axis, down)  195 us
    ppermute x75, starting transfers between devices, with_halo(): after = lax.ppermute(leading, axis, down)  97.7 us
    add x20, other arithmetic, chebyshev(): iterate = iterate + update  81.6 us
    unnamed x1, blocking collectives  41.3 us
    slice x57, local copies, waits for them, and re-layouts, with_halo(): last = lax.slice_in_dim(value, length - width, length, axis=dim)  40.7 us
    psum x1, blocking collectives, body(): residual_sq = lax.psum(jnp.sum(residual * residual), ('gx', 'gy', 'gz'))  38.4 us
    reshape x5, local copies, waits for them, and re-layouts, average_cells(): field.reshape(field.shape[0] // 2, 2, field.shape[1] // 2, 2, field.shape...  38 us
  transfers between devices with their start and end apart: 165, of which 84 were waited for; matrix products, arithmetic and copies ran while one was open for 30% of the time, Pallas kernels for 0%

commit v1 on v0

v1 whole, which is shorter than its diff:
```python
import functools

import jax
import jax.numpy as jnp
from jax import lax
from jax.experimental import pallas as pl
from jax.experimental.pallas import tpu as pltpu
from jax.sharding import PartitionSpec as P

LEVELS = 5
SWEEPS = 3
BOTTOM = 6
LANES = 128
TOP = 8

cheb_low = 0.25
cheb_high = 2.0
AXES = ("gx", "gy", "gz")
PER_LEVEL = 11


def ceil8(n):
    return (n + 7) // 8 * 8


def chebyshev_factors():
    centre = 0.5 * (cheb_high + cheb_low)
    half_width = 0.5 * (cheb_high - cheb_low)
    ratio = centre / half_width
    rho = 1.0 / ratio
    factors = [(0.0, 1.0 / centre)]
    for _ in range(SWEEPS - 1):
        new = 1.0 / (2.0 * ratio - rho)
        factors.append((new * rho, 2.0 * new / half_width))
        rho = new
    return factors


def iota(shape, dim):
    return lax.broadcasted_iota(jnp.int32, shape, dim)


def lane_roll(value, shift):
    if isinstance(shift, int):
        shift = shift % LANES
        return value if shift == 0 else pltpu.roll(value, shift, 1)
    return pltpu.roll(value, lax.rem(shift + LANES, LANES), 1)


def product(a, b):
    return jnp.dot(
        a, b, precision=lax.Precision.HIGHEST, preferred_element_type=jnp.float32
    )


def kernel(sizes, counts, rhs_ref, face_ref, cell_ref, sol_ref, res_ref, norm_ref, *scratch):
    deepest = LEVELS - 1
    levels = []
    at = 0
    for level in range(LEVELS):
        levels.append(scratch[at : at + PER_LEVEL])
        at += PER_LEVEL
    (stage, ysend, zsend, recv, cysend, czsend, crecv,
     gsend, gz_recv, gy_send, gy_recv, gx_recv, glob, whole,
     nsend, nz_recv, ny_recv, nx_recv,
     send_sem, recv_sem, csend_sem, crecv_sem, gsend_sem, grecv_sem,
     nsend_sem, nrecv_sem) = scratch[at:]
    place = [lax.axis_index(a) for a in AXES]
    factors = chebyshev_factors()
    low_of = iota((LANES, LANES), 0)
    high_of = iota((LANES, LANES), 1)
    pair_sum = jnp.where(low_of // 2 == high_of, 1.0, 0.0)
    pick_even = jnp.where(low_of == 2 * high_of, 1.0, 0.0)
    spread = jnp.where(low_of == high_of // 2, 1.0, 0.0)

    for dim in range(3):
        @pl.when(place[dim] == 0)
        def _():
            for slot in range(2):
                recv[slot, 2 * dim] = jnp.zeros_like(recv[slot, 2 * dim])

        @pl.when(place[dim] == counts[dim] - 1)
        def _():
            for slot in range(2):
                recv[slot, 2 * dim + 1] = jnp.zeros_like(recv[slot, 2 * dim + 1])
            for level in range(deepest):
                crecv[level, dim] = jnp.zeros_like(crecv[level, dim])

    def loop(n, body, init=0, unroll=None):
        if unroll is None:
            unroll = 2 if n % 2 == 0 else 1
        return lax.fori_loop(0, n, body, init, unroll=unroll)

    def clear(ref):
        def one(i, c):
            ref[i] = jnp.zeros(ref.shape[1:], jnp.float32)
            return c
        loop(ref.shape[0], one, unroll=1)

    stage[...] = jnp.zeros_like(stage)
    for level in range(deepest):
        for ref in levels[level][:2]:
            clear(ref)
    n = sizes[0]
    for ref in levels[0][2:]:
        clear(ref)

    xa, xb, f, dd, diag, inv, bx, by, bz, hz, cells = levels[0]

    def load(i, acc):
        value = rhs_ref[i]
        f[i, :, 0:n] = value
        bx[i, :, 0:n] = face_ref[0, i]
        by[i, 0:n, 0:n] = face_ref[1, i]
        bz[i, :, 0:n] = face_ref[2, i]
        cells[i, :, 0:n] = cell_ref[i]
        return acc
    loop(n, load)

    def source_square(i, acc):
        value = levels[0][2][i]
        return acc + value * value
    rhs_square = loop(n, source_square, jnp.zeros((n, LANES), jnp.float32))

    def transfer(nc, pick, matrix, scale, store):
        rows = ceil8(nc)

        def first(i, c):
            stage[i, 0:nc, :] = pick(i)
            return c
        loop(nc, first)
        chunk = nc
        while chunk * rows > 160 and chunk % 2 == 0:
            chunk //= 2

        def second(i, c):
            block = stage[pl.ds(i * chunk, chunk), 0:rows, :].reshape(chunk * rows, LANES)
            out = (product(block, matrix) * scale).reshape(chunk, rows, LANES)
            store(i * chunk, chunk, rows, out)
            return c
        loop(nc // chunk, second, unroll=1)

    def to(ref):
        def store(start, chunk, rows, out):
            ref[pl.ds(start, chunk), 0:rows, :] = out
        return store

    for level in range(deepest):
        nc = sizes[level + 1]
        _, _, _, _, _, _, bx, by, bz, hz, cells = levels[level]
        _, _, _, _, _, _, bx_c, by_c, bz_c, _, cells_c = levels[level + 1]

        def rows(ref, i, odd):
            return ref[i, pl.ds(odd, nc, stride=2), :]

        def four(ref, i):
            return (rows(ref, 2 * i, 0) + rows(ref, 2 * i, 1)) + (
                rows(ref, 2 * i + 1, 0) + rows(ref, 2 * i + 1, 1)
            )
        transfer(nc, lambda i: rows(bx, 2 * i, 0) + rows(bx, 2 * i, 1), pair_sum, 0.0625, to(bx_c))
        transfer(nc, lambda i: rows(by, 2 * i, 0) + rows(by, 2 * i + 1, 0), pair_sum, 0.0625, to(by_c))
        transfer(nc, lambda i: four(bz, i), pick_even, 0.0625, to(bz_c))
        transfer(nc, lambda i: four(cells, i), pair_sum, 0.125, to(cells_c))

    def coef_copy(level, dim):
        n = sizes[level]
        wide = ceil8(n)
        bx = levels[level][6]
        src = (
            bx.at[0, pl.ds(0, wide)],
            cysend.at[level, pl.ds(0, wide)],
            czsend.at[level, pl.ds(0, wide)],
        )[dim]
        return pltpu.make_async_remote_copy(
            src_ref=src,
            dst_ref=crecv.at[level, dim, pl.ds(0, wide)],
            send_sem=csend_sem.at[level, dim],
            recv_sem=crecv_sem.at[level, dim],
            device_id={AXES[dim]: jnp.maximum(place[dim] - 1, 0)},
            device_id_type=pl.DeviceIdType.MESH,
        )

    for level in range(deepest):
        n = sizes[level]
        _, _, _, _, _, _, bx, by, bz, hz, cells = levels[level]
        lane = iota((n, LANES), 1)

        def faces(i, acc):
            cysend[level, pl.ds(i, 1), :] = by[i, 0:1, :]
            return jnp.where(lane == i, lane_roll(bz[i, 0:n, :], i), acc)
        czsend[level, 0:n, :] = loop(n, faces, jnp.zeros((n, LANES), jnp.float32))
        for dim in range(3):
            @pl.when(place[dim] > 0)
            def _():
                coef_copy(level, dim).start()
    for level in range(deepest):
        for dim in range(3):
            @pl.when(place[dim] > 0)
            def _():
                coef_copy(level, dim).wait_send()

            @pl.when(place[dim] < counts[dim] - 1)
            def _():
                coef_copy(level, dim).wait_recv()
        n = sizes[level]
        wide = ceil8(n)
        _, _, _, _, diag, inv, bx, by, bz, hz, cells = levels[level]
        lane = iota((n, LANES), 1)
        bx[n, 0:wide, :] = crecv[level, 0, 0:wide, :]

        def finish(i, c):
            by[i, n : n + 1, :] = crecv[level, 1, pl.ds(i, 1), :]
            here = bz[i, 0:n, :]
            edge = lane_roll(crecv[level, 2, 0:n, :], n - 1 - i)
            upper = jnp.where(lane == n - 1, edge, lane_roll(here, -1))
            upper = jnp.where(lane < n, upper, 0.0)
            hz[i, 0:n, :] = upper
            total = bx[i, 0:n, :] + bx[i + 1, 0:n, :] + by[i, 0:n, :] + by[i, 1 : n + 1, :]
            total = total + here + upper + cells[i, 0:n, :]
            total = jnp.where(lane < n, total, 1.0)
            diag[i, 0:n, :] = jnp.where(lane < n, total, 0.0)
            inv[i, 0:n, :] = jnp.where(lane < n, 1.0 / total, 0.0)
            return c
        loop(n, finish)

    tally = [0]

    def face_copy(level, field, slot, dim, up):
        n = sizes[level]
        wide = ceil8(n)
        toward = jnp.minimum(place[dim] + 1, counts[dim] - 1) if up else jnp.maximum(place[dim] - 1, 0)
        part = 1 if up else 0
        if dim == 0:
            src = field.at[n if up else 1, pl.ds(TOP, wide)]
        else:
            src = (ysend if dim == 1 else zsend).at[part, pl.ds(0, wide)]
        which = 2 * dim + (0 if up else 1)
        return pltpu.make_async_remote_copy(
            src_ref=src,
            dst_ref=recv.at[slot, which, pl.ds(0, wide)],
            send_sem=send_sem.at[slot, which],
            recv_sem=recv_sem.at[slot, which],
            device_id={AXES[dim]: toward},
            device_id_type=pl.DeviceIdType.MESH,
        )

    def sweep_planes(level, field, make):
        n = sizes[level]
        lane = iota((n, LANES), 1)

        def one(i, accs):
            value = make(i)
            field[i + 1, TOP : TOP + n, :] = value
            ysend[0, pl.ds(i, 1), :] = value[0:1]
            ysend[1, pl.ds(i, 1), :] = value[n - 1 : n]
            turned = lane_roll(value, i - (n - 1))
            low = jnp.where(lane == lax.rem(i - n + 1 + LANES, LANES), turned, accs[0])
            high = jnp.where(lane == i, turned, accs[1])
            return low, high
        zero = jnp.zeros((n, LANES), jnp.float32)
        low, high = loop(n, one, (zero, zero))
        zsend[0, 0:n, :] = low
        zsend[1, 0:n, :] = high

    def exchange(level, field):
        slot = tally[0] % 2
        tally[0] += 1
        n = sizes[level]
        wide = ceil8(n)
        for dim in (1, 2, 0):
            last = counts[dim] - 1

            @pl.when(place[dim] < last)
            def _():
                face_copy(level, field, slot, dim, True).start()

            @pl.when(place[dim] > 0)
            def _():
                face_copy(level, field, slot, dim, False).start()
        for dim in (0, 2, 1):
            last = counts[dim] - 1

            @pl.when(place[dim] < last)
            def _():
                face_copy(level, field, slot, dim, True).wait_send()
                face_copy(level, field, slot, dim, False).wait_recv()

            @pl.when(place[dim] > 0)
            def _():
                face_copy(level, field, slot, dim, False).wait_send()
                face_copy(level, field, slot, dim, True).wait_recv()
        field[0, TOP : TOP + wide, :] = recv[slot, 0, 0:wide, :]
        field[n + 1, TOP : TOP + wide, :] = recv[slot, 1, 0:wide, :]
        _, _, f, _, diag, _, bx, by, bz, hz, _ = levels[level]
        lane = iota((n, LANES), 1)
        row = iota((n, LANES), 0)

        def remainder(i):
            here = field[i + 1, TOP : TOP + n, :]
            low_y = jnp.where(
                row == 0, recv[slot, 2, pl.ds(i, 1), :], field[i + 1, TOP - 1 : TOP - 1 + n, :]
            )
            high_y = jnp.where(
                row == n - 1, recv[slot, 3, pl.ds(i, 1), :], field[i + 1, TOP + 1 : TOP + 1 + n, :]
            )
            low_z = jnp.where(
                lane == 0, lane_roll(recv[slot, 4, 0:n, :], LANES - i), lane_roll(here, 1)
            )
            high_z = jnp.where(
                lane == n - 1,
                lane_roll(recv[slot, 5, 0:n, :], 2 * n - 2 - i),
                lane_roll(here, -1),
            )
            out = f[i, 0:n, :] - diag[i, 0:n, :] * here
            out = out + bx[i, 0:n, :] * field[i, TOP : TOP + n, :]
            out = out + bx[i + 1, 0:n, :] * field[i + 2, TOP : TOP + n, :]
            flow = by[i, 0:n, :] * low_y + by[i, 1 : n + 1, :] * high_y
            flow = flow + bz[i, 0:n, :] * low_z + hz[i, 0:n, :] * high_z
            return out + flow
        return remainder

    def chebyshev_sweep(level, old, new, factor):
        keep, gain = factor
        remainder = exchange(level, old)
        n = sizes[level]
        dd, inv = levels[level][3], levels[level][5]

        def make(i):
            step = gain * (inv[i, 0:n, :] * remainder(i))
            if keep:
                step = step + keep * dd[i, 0:n, :]
            dd[i, 0:n, :] = step
            return old[i + 1, TOP : TOP + n, :] + step
        sweep_planes(level, new, make)

    for level in range(deepest):
        n, nc = sizes[level], sizes[level + 1]
        xa, xb, f, dd, diag, inv = levels[level][:6]

        def begin(i):
            step = factors[0][1] * (inv[i, 0:n, :] * f[i, 0:n, :])
            dd[i, 0:n, :] = step
            return step
        sweep_planes(level, xa, begin)
        chebyshev_sweep(level, xa, xb, factors[1])
        chebyshev_sweep(level, xb, xa, factors[2])
        remainder = exchange(level, xa)

        def pick(i):
            xb[1, TOP : TOP + n, :] = remainder(2 * i) + remainder(2 * i + 1)
            return xb[1, pl.ds(TOP, nc, stride=2), :] + xb[1, pl.ds(TOP + 1, nc, stride=2), :]
        transfer(nc, pick, pair_sum, 0.125, to(levels[level + 1][2]))

    m = sizes[deepest]
    f_b, bx_b, by_b, bz_b, cells_b = [levels[deepest][k] for k in (2, 6, 7, 8, 10)]
    gsend[...] = jnp.zeros_like(gsend)
    for which, ref in enumerate((f_b, bx_b, by_b, bz_b, cells_b)):
        for i in range(m):
            start = (which * m + i) * m
            gsend[start : start + m, :] = lane_roll(ref[i, 0:m, :], place[2] * m)

    def line(dim, src, dst, ssem, rsem):
        total = counts[dim]

        def copy(off):
            return pltpu.make_async_remote_copy(
                src_ref=src,
                dst_ref=dst.at[place[dim]],
                send_sem=ssem.at[dim, off],
                recv_sem=rsem.at[dim, off],
                device_id={AXES[dim]: lax.rem(place[dim] + off, total)},
                device_id_type=pl.DeviceIdType.MESH,
            )
        for off in range(1, total):
            copy(off).start()
        dst[place[dim]] = src[...]
        for off in range(1, total):
            copy(off).wait()

    line(2, gsend, gz_recv, gsend_sem, grecv_sem)
    merged = gz_recv[0]
    for k in range(1, counts[2]):
        merged = merged + gz_recv[k]
    gy_send[...] = merged
    line(1, gy_send, gy_recv, gsend_sem, grecv_sem)
    line(0, gy_recv, gx_recv, gsend_sem, grecv_sem)

    tall = glob.shape[2]
    mx, my, mz = m * counts[0], m * counts[1], m * counts[2]
    glob[...] = jnp.zeros_like(glob)
    for which in range(5):
        for a in range(counts[0]):
            for b in range(counts[1]):
                for i in range(m):
                    start = (which * m + i) * m
                    glob[which, a * m + i, b * m : (b + 1) * m, :] = gx_recv[
                        a, b, start : start + m, :
                    ]
    lane = iota((tall, LANES), 1)
    row = iota((tall, LANES), 0)
    zero = jnp.zeros((tall, LANES), jnp.float32)
    for i in range(mx):
        hy = jnp.where(row < my - 1, pltpu.roll(glob[2, i], tall - 1, 0), 0.0)
        hz = jnp.where(lane < mz - 1, pltpu.roll(glob[3, i], LANES - 1, 1), 0.0)
        hx = glob[1, i + 1] if i + 1 < mx else zero
        glob[5, i] = hy
        glob[6, i] = hz
        glob[7, i] = glob[4, i] + glob[1, i] + hx + glob[2, i] + hy + glob[3, i] + hz

    def total(parts):
        acc = parts[0]
        for part in parts[1:]:
            acc = acc + part
        return jnp.sum(jnp.sum(acc, axis=0, keepdims=True), axis=1, keepdims=True)

    rest = [glob[0, i] for i in range(mx)]
    search = rest
    iterate = [zero] * mx
    norm_now = total([v * v for v in rest])
    for step in range(BOTTOM):
        applied = []
        for i in range(mx):
            v = search[i]
            out = glob[7, i] * v
            if i:
                out = out - glob[1, i] * search[i - 1]
            if i + 1 < mx:
                out = out - glob[1, i + 1] * search[i + 1]
            out = out - glob[2, i] * pltpu.roll(v, 1, 0) - glob[5, i] * pltpu.roll(v, tall - 1, 0)
            out = out - glob[3, i] * pltpu.roll(v, 1, 1) - glob[6, i] * pltpu.roll(v, LANES - 1, 1)
            applied.append(out)
        size = norm_now / total([a * b for a, b in zip(search, applied)])
        iterate = [e + size * v for e, v in zip(iterate, search)]
        if step + 1 < BOTTOM:
            rest = [r - size * q for r, q in zip(rest, applied)]
            norm_next = total([v * v for v in rest])
            ratio = norm_next / norm_now
            search = [r + ratio * v for r, v in zip(rest, search)]
            norm_now = norm_next
    for i in range(mx):
        whole[i] = iterate[i]
    below = levels[deepest][3]
    lane = iota((m, LANES), 1)
    for i in range(m):
        plane = whole[place[0] * m + i]
        plane = pltpu.roll(plane, lax.rem(tall - place[1] * m + tall, tall), 0)
        plane = pltpu.roll(plane, lax.rem(LANES - place[2] * m + LANES, LANES), 1)
        below[i, 0:m, :] = jnp.where(lane < m, plane[0:m], 0.0)

    coarse = lambda i: below[i, 0:m, :]
    for level in reversed(range(deepest)):
        n, nc = sizes[level], sizes[level + 1]
        xa, xb = levels[level][:2]

        def add(start, chunk, rows, out):
            for k in range(chunk):
                for odd_x in range(2):
                    plane = 2 * (start + k) + odd_x + 1
                    for odd_y in range(2):
                        at_rows = pl.ds(TOP + odd_y, nc, stride=2)
                        xa[plane, at_rows, :] = xa[plane, at_rows, :] + out[k, 0:nc]
        transfer(nc, coarse, spread, 1.0, add)
        sweep_planes(level, xa, lambda i: xa[i + 1, TOP : TOP + n, :])
        chebyshev_sweep(level, xa, xb, factors[0])
        chebyshev_sweep(level, xb, xa, factors[1])
        chebyshev_sweep(level, xa, xb, factors[2])
        coarse = functools.partial(lambda ref, count, i: ref[i + 1, TOP : TOP + count, :], xb, n)

    n = sizes[0]
    xa, xb = levels[0][:2]
    remainder = exchange(0, xb)

    def finish(i, acc):
        out = remainder(i)
        sol_ref[i] = xb[i + 1, TOP : TOP + n, 0:n]
        res_ref[i] = out[:, 0:n]
        return acc + out * out
    res_square = loop(n, finish, jnp.zeros((n, LANES), jnp.float32))
    nsend[0, 0:1, :] = jnp.sum(res_square, axis=0, keepdims=True)
    nsend[0, 1:2, :] = jnp.sum(rhs_square, axis=0, keepdims=True)
    nsend[0, 2:8, :] = jnp.zeros((6, LANES), jnp.float32)
    for step, (dim, got) in enumerate(((2, nz_recv), (1, ny_recv), (0, nx_recv))):
        line(dim, nsend.at[step], got, nsend_sem, nrecv_sem)
        acc = got[0]
        for k in range(1, counts[dim]):
            acc = acc + got[k]
        if step < 2:
            nsend[step + 1] = acc
    sums = jnp.sum(acc, axis=1, keepdims=True)
    norm_ref[...] = jnp.broadcast_to(jnp.sqrt(sums[0:1] / sums[1:2]), norm_ref.shape)


def body(counts, right_side, face_coef, absorption):
    n = right_side.shape[0]
    sizes = [n >> level for level in range(LEVELS)]
    f32 = jnp.float32
    scratch = []
    for size in sizes:
        wide = ceil8(size)
        flat = pltpu.VMEM((size, wide, LANES), f32)
        field = pltpu.VMEM((size + 2, wide + 2 * TOP, LANES), f32)
        scratch += [field, field, flat, flat, flat, flat]
        scratch += [
            pltpu.VMEM((size + 1, wide, LANES), f32),
            pltpu.VMEM((size, wide + 8, LANES), f32),
            flat, flat, flat,
        ]
    wide = ceil8(n)
    half = ceil8(n // 2)
    m = sizes[-1]
    packed = ceil8(5 * m * m)
    tall = (m * counts[1] + 8) // 8 * 8
    most = max(counts)
    scratch += [
        pltpu.VMEM((n // 2, half, LANES), f32),
        pltpu.VMEM((2, wide, LANES), f32),
        pltpu.VMEM((2, wide, LANES), f32),
        pltpu.VMEM((2, 6, wide, LANES), f32),
        pltpu.VMEM((LEVELS - 1, wide, LANES), f32),
        pltpu.VMEM((LEVELS - 1, wide, LANES), f32),
        pltpu.VMEM((LEVELS - 1, 3, wide, LANES), f32),
        pltpu.VMEM((packed, LANES), f32),
        pltpu.VMEM((counts[2], packed, LANES), f32),
        pltpu.VMEM((packed, LANES), f32),
        pltpu.VMEM((counts[1], packed, LANES), f32),
        pltpu.VMEM((counts[0], counts[1], packed, LANES), f32),
        pltpu.VMEM((8, m * counts[0], tall, LANES), f32),
        pltpu.VMEM((m * counts[0], tall, LANES), f32),
        pltpu.VMEM((3, 8, LANES), f32),
        pltpu.VMEM((counts[2], 8, LANES), f32),
        pltpu.VMEM((counts[1], 8, LANES), f32),
        pltpu.VMEM((counts[0], 8, LANES), f32),
        pltpu.SemaphoreType.DMA((2, 6)),
        pltpu.SemaphoreType.DMA((2, 6)),
        pltpu.SemaphoreType.DMA((LEVELS - 1, 3)),
        pltpu.SemaphoreType.DMA((LEVELS - 1, 3)),
        pltpu.SemaphoreType.DMA((3, most)),
        pltpu.SemaphoreType.DMA((3, most)),
        pltpu.SemaphoreType.DMA((3, most)),
        pltpu.SemaphoreType.DMA((3, most)),
    ]
    vmem = pl.BlockSpec(memory_space=pltpu.VMEM)
    answer, residual, norm = pl.pallas_call(
        functools.partial(kernel, sizes, counts),
        out_shape=(
            jax.ShapeDtypeStruct(right_side.shape, f32),
            jax.ShapeDtypeStruct(right_side.shape, f32),
            jax.ShapeDtypeStruct((8, LANES), f32),
        ),
        in_specs=[vmem] * 3,
        out_specs=(vmem,) * 3,
        scratch_shapes=scratch,
        compiler_params=pltpu.CompilerParams(
            has_side_effects=True, vmem_limit_bytes=60 * 1024 * 1024
        ),
        name="vcycle",
    )(right_side, face_coef, absorption)
    return answer, residual, norm[0, 0]


def solution(mesh):
    counts = tuple(mesh.shape[a] for a in AXES)
    return jax.shard_map(
        functools.partial(body, counts),
        mesh=mesh,
        in_specs=(P("gx", "gy", "gz"), P(None, "gx", "gy", "gz"), P("gx", "gy", "gz")),
        out_specs=(P("gx", "gy", "gz"), P("gx", "gy", "gz"), P()),
        check_vma=False,
    )
```

time: 1300 us -> 198 us (0.15); the launches traced: 1280 us -> 198 us
  starting transfers between devices: 344 us -> 0 us
  local copies, waits for them, and re-layouts: 345 us -> 4.66 us
  other arithmetic: 259 us -> 0 us
  waiting for transfers between devices: 232 us -> 0 us
  Pallas kernels: 0 us -> 193 us
  blocking collectives: 79.7 us -> 0 us
  between operations: 21.3 us -> 0.64 us
    ppermute x165 -> x0, starting transfers between devices: 344 us -> none  [the longest x75 226 us: with_halo(): before = lax.ppermute(last, axis, up)]
    ppermute x165 -> x0, waiting for transfers between devices: 232 us -> none  [the longest x75 195 us: with_halo(): after = lax.ppermute(leading, axis, down)]
    pallas_call x0 -> x1, Pallas kernels: none -> 193 us  [body(): pl.pallas_call(functools.partial(kernel, sizes, counts), out_shape=(jax.S...]
    reduce_sum x33 -> x0, other arithmetic: 114 us -> none  [the longest x8 35.4 us: average_cells(): return jnp.sum(blocks, axis=(1, 3, 5)) * 0.125]
    add x30 -> x0, other arithmetic: 91.5 us -> none  [the longest x20 81.6 us: chebyshev(): iterate = iterate + update]
    slice x86 -> x1, local copies, waits for them, and re-layouts: 84.8 us -> 1.19 us  [body(): return (answer, residual, norm[0, 0])]
    another operation x13 -> x0, local copies, waits for them, and re-layouts: 69.9 us -> none  [the longest x4 22.8 us: average_faces(): along_x = faces[0].reshape(halves)[:, 0]]
    reshape x12 -> x0, local copies, waits for them, and re-layouts: 68.7 us -> none  [the longest x5 38 us: average_cells(): field.reshape(field.shape[0] // 2, 2, field.shape[1] // 2, 2, field.shape...]
  transfers between devices with their start and end apart: 165 -> 0, of which waited for: 84 -> 0; matrix products, arithmetic and copies ran while one was open for 30% -> 0% of each run, Pallas kernels for 0% -> 0%
where the time goes in v1:
time: 198 us
  Pallas kernels  193 us (97%)
  local copies, waits for them, and re-layouts  4.66 us (2%)
    pallas_call x1, Pallas kernels, body(): pl.pallas_call(functools.partial(kernel, sizes, counts), out_shape=(jax.S...  193 us

profile of v1, /device:TPU:0, one launch (start us, length us, event | category | flops | bytes accessed | tf_op | source)
XLA Modules:
  0.0 197.8 jit_solution(9108077338703666147)
XLA Ops:
  0.6 192.5 %vcycle.1 = (f32[48,48,48]{2,1,0:T(8,128)}, f32[48,48,48]{2,1,0:T(8,128)}, f32[8,128]{1,0:T(8,128)}) custom-call(f32[48,48,48]{2,1,0:T(8,128)} %rhs_ref.1, f32[3,48,48,48]{3,2,1,0:T(8,128)} %face_ref.1, f32[48,48,48]{2,1,0:T(8,128)} %cell_ref.1), custom_call_target="tpu_custom_call" | custom-call | tf_op jit(solution)/shard_map/vcycle/pallas_call | solution.py:543
  193.2 1.2 slice.3
  194.3 0.0 copy-start
  194.4 2.5 %copy.8 = f32[48,48,48]{2,1,0:T(8,128)} copy(f32[48,48,48]{2,1,0:T(8,128)} %get-tuple-element.12) | data formatting | bytes 884736
  196.8 0.0 copy-done
  196.8 1.0 copy.9
Async XLA Ops:
  194.3 2.5 %copy-start = (f32[48,48,48]{2,1,0:T(8,128)S(1)}, f32[48,48,48]{2,1,0:T(8,128)}, u32[]{:S(2)}) copy-start(f32[48,48,48]{2,1,0:T(8,128)} %get-tuple-element.13) | copy-start | bytes 1327108

commit v2 on v1

--- a/solution.py
+++ b/solution.py
@@ -88,7 +88,7 @@
 
     def loop(n, body, init=0, unroll=None):
         if unroll is None:
-            unroll = 2 if n % 2 == 0 else 1
+            unroll = next(u for u in (4, 3, 2, 1) if n % u == 0)
         return lax.fori_loop(0, n, body, init, unroll=unroll)
 
     def clear(ref):
@@ -347,8 +347,10 @@
         remainder = exchange(level, xa)
 
         def pick(i):
-            xb[1, TOP : TOP + n, :] = remainder(2 * i) + remainder(2 * i + 1)
-            return xb[1, pl.ds(TOP, nc, stride=2), :] + xb[1, pl.ds(TOP + 1, nc, stride=2), :]
+            xb[i + 1, TOP : TOP + n, :] = remainder(2 * i) + remainder(2 * i + 1)
+            return (
+                xb[i + 1, pl.ds(TOP, nc, stride=2), :] + xb[i + 1, pl.ds(TOP + 1, nc, stride=2), :]
+            )
         transfer(nc, pick, pair_sum, 0.125, to(levels[level + 1][2]))
 
     m = sizes[deepest]

time: 198 us -> 175 us (0.88)
  Pallas kernels: 193 us -> 169 us
    pallas_call x1, Pallas kernels: 193 us -> 169 us  [body(): pl.pallas_call(functools.partial(kernel, sizes, counts), out_shape=(jax.S...]
where the time goes in v2:
time: 175 us
  Pallas kernels  169 us (97%)
  local copies, waits for them, and re-layouts  4.66 us (3%)
    pallas_call x1, Pallas kernels, body(): pl.pallas_call(functools.partial(kernel, sizes, counts), out_shape=(jax.S...  169 us

profile of v2, /device:TPU:0, one launch (start us, length us, event | category | flops | bytes accessed | tf_op | source)
XLA Modules:
  0.0 174.8 jit_solution(11858969680559156274)
XLA Ops:
  0.6 169.5 %vcycle.1 = (f32[48,48,48]{2,1,0:T(8,128)}, f32[48,48,48]{2,1,0:T(8,128)}, f32[8,128]{1,0:T(8,128)}) custom-call(f32[48,48,48]{2,1,0:T(8,128)} %rhs_ref.1, f32[3,48,48,48]{3,2,1,0:T(8,128)} %face_ref.1, f32[48,48,48]{2,1,0:T(8,128)} %cell_ref.1), custom_call_target="tpu_custom_call" | custom-call | tf_op jit(solution)/shard_map/vcycle/pallas_call | solution.py:545
  170.1 1.2 slice.3
  171.3 0.0 copy-start
  171.3 2.5 %copy.8 = f32[48,48,48]{2,1,0:T(8,128)} copy(f32[48,48,48]{2,1,0:T(8,128)} %get-tuple-element.12) | data formatting | bytes 884736
  173.7 0.0 copy-done
  173.7 1.0 copy.9
Async XLA Ops:
  171.3 2.5 %copy-start = (f32[48,48,48]{2,1,0:T(8,128)S(1)}, f32[48,48,48]{2,1,0:T(8,128)}, u32[]{:S(2)}) copy-start(f32[48,48,48]{2,1,0:T(8,128)} %get-tuple-element.13) | copy-start | bytes 1327108
